TPU v7x, 32 devices: a whole 2x2x4 slice. The times are simulated.
32 devices in a mesh: seq: 4 (over x, core), mp: 8 (over z, y).
Axes of the slice: x: 2, y: 2, z: 4, core: 2. Of those that a mesh axis runs over, the one named last changes fastest.
Arguments:
- byte_states: bfloat16 [4, 4096, 1024], P('seq', 'mp'), may hold values from -312 to 312
- patch_latents: bfloat16 [4, 1024, 4096], P(None, 'seq', 'mp'), may hold values from -6 to 6
- patch_lengths: int32 [4, 1024], P('seq'), may hold values from 1 to 12, 4096 in all within a row
- w_down: bfloat16 [4096, 1024], replicated, may hold values from -0.09375 to 0.09375
- kv_gain: bfloat16 [1024], replicated, may hold values from 0.25 to 1.75
- w_query: bfloat16 [1024, 1024], replicated, may hold values from -0.375 to 0.375
- w_key: bfloat16 [1024, 1024], replicated, may hold values from -0.1875 to 0.1875
- w_value: bfloat16 [1024, 1024], replicated, may hold values from -0.1875 to 0.1875
- w_out: bfloat16 [1024, 1024], replicated, may hold values from -0.375 to 0.375
- out_gain: bfloat16 [1024], replicated, may hold values from 0.25 to 1.75
Outputs:
- decoded: bfloat16 [4, 4096, 1024], P('seq', 'mp')
Inputs may be any that keep to these rules, and one draw needn't show every extreme that they name: patch_lengths[s] lists the lengths of the 1024 patches of sequence s in order; they sum to 4096 and the longest is exactly 12.
All inputs are finite; a program needn't handle non-finite values.
Results may differ from a plain program's by a relative error of at most 0.0076.
Values may be sent and summed in bfloat16 or wider, within the bound.
A program may use at most 128 MiB of HBM per device.

v0:
```python
import math
import jax
import jax.numpy as jnp
from jax import lax
from jax.sharding import PartitionSpec as P

HEADS = 16
HEAD_DIM = 64
NEG_FLOOR = -1e30


def rms_norm(values, gain_row):
    mean_square = jnp.mean(values * values, axis=-1, keepdims=True)
    return values * lax.rsqrt(mean_square + 1e-05) * gain_row.astype(jnp.float32)


def fold_block(fold_state, query_part, position_part, key_block, value_block, start_block):
    row_max, denominator, accumulated = fold_state
    scale_factor = 1.0 / math.sqrt(HEAD_DIM)
    scores = (
        jnp.einsum("rhd,khd->hrk", query_part, key_block, preferred_element_type=jnp.float32)
        * scale_factor
    )
    allowed = start_block[None, None, :] <= position_part[None, :, None]
    masked = jnp.where(allowed, scores, NEG_FLOOR)
    new_max = jnp.maximum(row_max, jnp.max(masked, axis=-1))
    raised = jnp.where(allowed, jnp.exp(masked - new_max[..., None]), 0.0)
    correction = jnp.exp(row_max - new_max)
    denominator = denominator * correction + jnp.sum(raised, axis=-1)
    accumulated = accumulated * correction[..., None] + jnp.einsum(
        "hrk,khd->hrd", raised.astype(jnp.bfloat16), value_block, preferred_element_type=jnp.float32
    )
    return (new_max, denominator, accumulated)


def make_folder(query_halves, position_halves, starts):

    def folder(running, arrived_piece, piece_start):
        key_piece, value_piece = arrived_piece
        piece_rows = key_piece.shape[0]
        step_rows = math.gcd(piece_rows, 512)

        def one_block(block_index, fold_state):
            offset = block_index * step_rows
            key_block = lax.dynamic_slice_in_dim(key_piece, offset, step_rows, 0).reshape(
                step_rows, HEADS, HEAD_DIM
            )
            value_block = lax.dynamic_slice_in_dim(value_piece, offset, step_rows, 0).reshape(
                step_rows, HEADS, HEAD_DIM
            )
            start_block = lax.dynamic_slice_in_dim(starts, offset, step_rows, 0)
            updated = []
            for part_index in range(2):
                part_state = tuple((member[part_index] for member in fold_state))

                def advance(inner_state, part_index=part_index):
                    return fold_block(
                        inner_state,
                        query_halves[part_index],
                        position_halves[part_index],
                        key_block,
                        value_block,
                        start_block,
                    )

                def remain(inner_state):
                    return inner_state

                needed = start_block[0] <= position_halves[part_index][-1]
                updated.append(lax.cond(needed, advance, remain, part_state))
            return tuple((jnp.stack([updated[0][slot], updated[1][slot]]) for slot in range(3)))

        return lax.fori_loop(0, piece_rows // step_rows, one_block, running)

    return folder


def per_device(
    byte_states,
    patch_latents,
    patch_lengths,
    w_down,
    kv_gain,
    w_query,
    w_key,
    w_value,
    w_out,
    out_gain,
):
    my_rank = lax.axis_index("mp")
    tokens_here = byte_states.shape[1]
    half_rows = tokens_here // 2
    regrouped = lax.all_to_all(
        lax.all_to_all(patch_latents, "seq", split_axis=0, concat_axis=1, tiled=True),
        "mp",
        split_axis=1,
        concat_axis=2,
        tiled=True,
    )
    projected = jnp.dot(regrouped[0], w_down, preferred_element_type=jnp.float32)
    patch_normed = rms_norm(projected, kv_gain).astype(jnp.bfloat16)
    lengths = patch_lengths[0]
    starts = jnp.cumsum(lengths) - lengths
    own_rows = byte_states[0]
    local_offsets = jnp.arange(half_rows, dtype=jnp.int32)
    first_position = my_rank * tokens_here
    position_halves = jnp.stack(
        [first_position + local_offsets, first_position + half_rows + local_offsets]
    )
    queries = jnp.dot(own_rows, w_query, preferred_element_type=jnp.float32).astype(jnp.bfloat16)
    query_halves = queries.reshape(2, half_rows, HEADS, HEAD_DIM)
    initial = (
        jnp.full((2, HEADS, half_rows), NEG_FLOOR, jnp.float32),
        jnp.zeros((2, HEADS, half_rows), jnp.float32),
        jnp.zeros((2, HEADS, half_rows, HEAD_DIM), jnp.float32),
    )
    key_rows = jnp.dot(patch_normed, w_key, preferred_element_type=jnp.float32).astype(jnp.bfloat16)
    value_rows = jnp.dot(patch_normed, w_value, preferred_element_type=jnp.float32).astype(
        jnp.bfloat16
    )
    folder = make_folder(query_halves, position_halves, starts)
    row_max, denominator, accumulated = folder(
        initial,
        (
            lax.all_gather(key_rows, "mp", axis=0, tiled=True),
            lax.all_gather(value_rows, "mp", axis=0, tiled=True),
        ),
        jnp.int32(0),
    )
    summed = accumulated / denominator[..., None]
    head_out = (
        jnp.transpose(summed, (0, 2, 1, 3))
        .reshape(tokens_here, HEADS * HEAD_DIM)
        .astype(jnp.bfloat16)
    )
    residual = own_rows.astype(jnp.float32) + jnp.dot(
        head_out, w_out, preferred_element_type=jnp.float32
    )
    decoded = rms_norm(residual, out_gain).astype(jnp.bfloat16)
    return decoded[None]


def solution(mesh):
    return jax.shard_map(
        per_device,
        mesh=mesh,
        in_specs=(
            P("seq", "mp", None),
            P(None, "seq", "mp"),
            P("seq", None),
            P(),
            P(),
            P(),
            P(),
            P(),
            P(),
            P(),
        ),
        out_specs=P("seq", "mp", None),
        check_vma=False,
    )
```

profile of v0, /device:TPU:16, one launch (start us, length us, event | category | flops | bytes accessed | tf_op | source)
XLA Modules:
  0.0 283.9 jit_solution(9395675272807082795)
XLA Ops:
  6.5 18.0 %all_to_all.27 = bf16[4,256,512]{2,1,0:T(8,128)(2,1)S(1)} all-to-all(bf16[4,256,512]{2,1,0:T(8,128)(2,1)} %param.17), channel_id=1, replica_groups=mesh['seq'=4,'mp'=8] {'seq'}, dimensions={0} | all-to-all | bytes 2097152 | tf_op jit(solution)/shard_map/all_to_all | solution.py:94
  24.6 3.0 %copy.45 = bf16[1,1024,512]{2,0,1:T(2,128)(2,1)} copy(bf16[1,1024,512]{2,1,0:T(8,128)(2,1)S(1)} %bitcast.101) | data formatting | bytes 2097152 | tf_op jit(solution)/shard_map/all_to_all | solution.py:94
  28.1 8.0 %reduce.2 = bf16[1024,512]{1,0:T(8,128)(2,1)S(1)} reduce(bf16[1024,1,512]{2,1,0:T(2,128)(2,1)} %bitcast.98, bf16[]{:T(256)} %broadcast.104), dimensions={1}, to_apply=%bitcast.78.reduce_sub_computation | reduce | bytes 2097154
  37.7 6.2 %all-to-all-start.1 = ((bf16[8,2,32768]{2,1,0:T(2,128)(2,1)}), bf16[8,2,32768]{2,1,0:T(2,128)(2,1)S(1)}, u32[]{:S(2)}, u32[]{:S(2)}) async-start(bf16[8,2,32768]{2,1,0:T(2,128)(2,1)} %reshape.138), calls=%async_computation.1 | async-start | bytes 2097152 | tf_op jit(solution)/shard_map/all_to_all | solution.py:93
  43.9 22.3 %all-to-all-done.1 = bf16[8,2,32768]{2,1,0:T(2,128)(2,1)S(1)} async-done(((bf16[8,2,32768]{2,1,0:T(2,128)(2,1)}), bf16[8,2,32768]{2,1,0:T(2,128)(2,1)S(1)}, u32[]{:S(2)}, u32[]{:S(2)}) %all-to-all-start.1) | async-done | bytes 1048608 | tf_op jit(solution)/shard_map/all_to_all | solution.py:93
  66.1 3.4 %reshape.139 = bf16[1024,1,512]{2,1,0:T(2,128)(2,1)} reshape(bf16[8,2,32768]{2,1,0:T(2,128)(2,1)S(1)} %all-to-all-done.1) | data formatting | bytes 2097152
  74.0 4.9 %multiply_reduce_fusion.1 = (f32[128]{0:T(128)S(1)}, f32[128,1024]{1,0:T(8,128)S(1)}) fusion(bf16[128,4096]{0,1:T(8,128)(2,1)S(1)} %bitcast.99, bf16[4096,1024]{1,0:T(8,128)(2,1)} %param.19), kind=kOutput, calls=%fused_computation.58 | convolution fusion | flops 1074003840 | bytes 9961984 | tf_op jit(solution)/shard_map/dot_general | solution.py:100
  81.2 3.0 %convolution_convert_fusion.1 = bf16[128,1024]{1,0:T(8,128)(2,1)} fusion(bf16[1024,1024]{1,0:T(8,128)(2,1)} %param.23, f32[128,1024]{1,0:T(8,128)} %copy-done.7, f32[1024]{0:T(1024)S(1)} %convert_element_type.60, f32[128]{0:T(128)S(1)} %add_rsqrt_fusion.1), kind=kOutput, calls=%fused_computation.52 | convolution fusion | flops 268959744 | bytes 2888192 | tf_op jit(solution)/shard_map/dot_general | solution.py:118
  84.6 3.2 %convolution_convert_fusion = bf16[512,1024]{1,0:T(8,128)(2,1)S(1)} fusion(bf16[1024,1024]{1,0:T(8,128)(2,1)} %param.21, bf16[1,512,1024]{2,1,0:T(8,128)(2,1)} %param.16), kind=kOutput, calls=%fused_computation.51 | convolution fusion | flops 1074266112 | bytes 4194304 | tf_op jit(solution)/shard_map/dot_general | solution.py:110
  90.1 3.6 %copy.36 = bf16[2,256,16,64]{1,3,2,0:T(8,128)(2,1)} copy(bf16[2,256,16,64]{3,2,1,0:T(8,128)(2,1)} %reshape.136) | data formatting | bytes 2097152 | tf_op jit(solution)/shard_map/while | solution.py:73
  93.8 36.8 %all-gather.3.cloned.1.call-done = bf16[1024,1024]{1,0:T(8,128)(2,1)} async-done(((bf16[128,1024]{1,0:T(8,128)(2,1)}), bf16[1024,1024]{1,0:T(8,128)(2,1)}) %all-gather.3.cloned.1.call-update) | async-done | bytes 2097168 | tf_op jit(solution)/shard_map/all_gather | solution.py:125
  130.6 49.8 %all-gather.5.cloned.1.call-done = bf16[1024,1024]{1,0:T(8,128)(2,1)} async-done(((bf16[128,1024]{1,0:T(8,128)(2,1)}), bf16[1024,1024]{1,0:T(8,128)(2,1)}) %all-gather.5.cloned.1.call-update) | async-done | bytes 2097168 | tf_op jit(solution)/shard_map/all_gather | solution.py:126
  182.0 88.0 %while.17 = (s32[]{:T(128)}, f32[2,16,256]{2,1,0:T(8,128)S(1)}, f32[2,16,256]{2,1,0:T(8,128)S(1)}, f32[2,16,256,64]{2,3,1,0:T(8,128)}, s32[1024]{0:T(1024)S(1)},...) while((s32[]{:T(128)}, f32[2,16,256]{2,1,0:T(8,128)S(1)}, ...), condition=%wide.region_12.13_spmd, body=%wide.region_3.12_spmd.sunk | while | flops 1130135552 | bytes 103557752 | solution.py:73
  185.2 3.1 %slice_bitcast_fusion.9 = (f32[16,256,64]{1,2,0:T(8,128)}, f32[16,256,64]{1,2,0:T(8,128)}) fusion(f32[2,16,256,64]{2,3,1,0:T(8,128)} %get-tuple-element.503), kind=kLoop, calls=%fused_computation.38.clone.1 | loop fusion | bytes 4194304 | tf_op jit(solution)/shard_map/while/body/eval_jaxpr/squeeze | solution.py:54
  188.3 3.0 %constant_dynamic-slice_fusion.3 = (bf16[512,1024]{1,0:T(8,128)(2,1)}, bf16[512,1024]{1,0:T(8,128)(2,1)}) fusion(bf16[1024,1024]{1,0:T(8,128)(2,1)} %get-tuple-element.521, s32[]{:T(128)S(6)} %select_n.71, bf16[1024,1024]{1,0:T(8,128)(2,1)} %get-tuple-element.520), kind=kLoop, calls=%fused_computation.45.clone.1 | loop fusion | bytes 4194308 | tf_op jit(solution)/shard_map/while/body/eval_jaxpr/dynamic_slice | solution.py:48
  195.8 11.8 %conditional.4 = (f32[1,16,256]{2,1,0:T(8,128)}, f32[1,16,256]{2,1,0:T(8,128)S(1)}, f32[1,16,256,64]{2,3,1,0:T(8,128)}) conditional(s32[]{:T(128)} %bitcast.87, (f32[16,256]{1,0:T(8,128)}, f32[16,256]{1,0:T(8,128)S(1)}, f32[16,256,64]{1,2,0:T(8,128)}) %tuple.129, (s32[512]{0:T(512)S(1)}, s32[256]{0:T(256)S(1)}, bf16[2,256,16,64]{1,3,2,0:T(8,128)(2,1)}, ...), branch_computations={%region_8.8_spmd, %region_9.0_spmd} | conditional | flops 564797440 | bytes 43224172 | solution.py:70
  199.5 3.2 %fusion.20 = f32[16,256]{1,0:T(8,128)S(1)} fusion(f32[16,256,512]{2,1,0:T(8,128)S(1)} %get-tuple-element.368, f32[16,256]{1,0:T(8,128)} %max.5, pred[256,512]{1,0:T(8,128)(4,1)S(1)} %broadcast_compare_fusion.1), kind=kLoop, calls=%fused_computation.22 | loop fusion | flops 10481664 | bytes 8552448 | tf_op jit(solution)/shard_map/while/body/eval_jaxpr/cond/branch_1_fun/reduce_sum | solution.py:29
  203.5 3.1 %fusion.27 = f32[1,16,256,64]{2,3,1,0:T(8,128)S(1)} fusion(bf16[512,16,64]{0,2,1:T(8,128)(2,1)S(1)} %copy-done.5, f32[16,256,512]{2,1,0:T(8,128)S(1)} %get-tuple-element.368, f32[16,256]{1,0:T(8,128)} %max.5, pred[256,512]{1,0:T(8,128)(4,1)S(1)} %broadcast_compare_fusion.1, f32[16,256,64]{1,2,0:T(8,128)S(1)} %copy-done.3, f32[16,256]{1,0:T(8,128)S(1)} %get-tuple-element.364), kind=kOutput, calls=%fused_computation.26 | convolution fusion | flops 279445504 | bytes 11698176 | tf_op jit(solution)/shard_map/while/body/eval_jaxpr/cond/branch_1_fun/hrk,khd->hrd/dot_general | solution.py:30
  210.3 11.8 %conditional.5 = (f32[1,16,256]{2,1,0:T(8,128)}, f32[1,16,256]{2,1,0:T(8,128)S(1)}, f32[1,16,256,64]{2,3,1,0:T(8,128)}) conditional(s32[]{:T(128)} %bitcast.90, (f32[16,256]{1,0:T(8,128)}, f32[16,256]{1,0:T(8,128)S(1)}, f32[16,256,64]{1,2,0:T(8,128)}) %tuple.131, (s32[512]{0:T(512)S(1)}, s32[256]{0:T(256)S(1)}, bf16[2,256,16,64]{1,3,2,0:T(8,128)(2,1)}, ...), branch_computations={%region_4.4_spmd, %region_5.0_spmd} | conditional | flops 564797440 | bytes 43224172 | solution.py:70
  214.0 3.2 %fusion.2 = f32[16,256]{1,0:T(8,128)S(1)} fusion(f32[16,256,512]{2,1,0:T(8,128)S(1)} %get-tuple-element.366, f32[16,256]{1,0:T(8,128)} %max.4, pred[256,512]{1,0:T(8,128)(4,1)S(1)} %broadcast_compare_fusion), kind=kLoop, calls=%fused_computation.4 | loop fusion | flops 10481664 | bytes 8552448 | tf_op jit(solution)/shard_map/while/body/eval_jaxpr/cond/branch_1_fun/reduce_sum | solution.py:29
  218.0 3.1 %fusion.9 = f32[1,16,256,64]{2,3,1,0:T(8,128)S(1)} fusion(bf16[512,16,64]{0,2,1:T(8,128)(2,1)S(1)} %copy-done.6, f32[16,256,512]{2,1,0:T(8,128)S(1)} %get-tuple-element.366, f32[16,256]{1,0:T(8,128)} %max.4, pred[256,512]{1,0:T(8,128)(4,1)S(1)} %broadcast_compare_fusion, f32[16,256,64]{1,2,0:T(8,128)S(1)} %copy-done.1, f32[16,256]{1,0:T(8,128)S(1)} %get-tuple-element.362), kind=kOutput, calls=%fused_computation.8 | convolution fusion | flops 279445504 | bytes 11698176 | tf_op jit(solution)/shard_map/while/body/eval_jaxpr/cond/branch_1_fun/hrk,khd->hrd/dot_general | solution.py:30
  222.9 3.1 %pad_maximum_fusion.8 = f32[2,16,256,64]{2,3,1,0:T(8,128)} fusion(f32[1,16,256,64]{2,3,1,0:T(8,128)} %get-tuple-element.472, f32[1,16,256,64]{2,3,1,0:T(8,128)} %get-tuple-element.473), kind=kLoop, calls=%fused_computation.36.clone.1 | loop fusion | flops 524288 | bytes 4194304 | tf_op jit(solution)/shard_map/while/body/eval_jaxpr/stack | solution.py:71
  229.2 3.1 %slice_bitcast_fusion.9 = (f32[16,256,64]{1,2,0:T(8,128)}, f32[16,256,64]{1,2,0:T(8,128)}) fusion(f32[2,16,256,64]{2,3,1,0:T(8,128)} %get-tuple-element.503), kind=kLoop, calls=%fused_computation.38.clone.1 | loop fusion | bytes 4194304 | tf_op jit(solution)/shard_map/while/body/eval_jaxpr/squeeze | solution.py:54
  232.3 3.0 %constant_dynamic-slice_fusion.3 = (bf16[512,1024]{1,0:T(8,128)(2,1)}, bf16[512,1024]{1,0:T(8,128)(2,1)}) fusion(bf16[1024,1024]{1,0:T(8,128)(2,1)} %get-tuple-element.521, s32[]{:T(128)S(6)} %select_n.71, bf16[1024,1024]{1,0:T(8,128)(2,1)} %get-tuple-element.520), kind=kLoop, calls=%fused_computation.45.clone.1 | loop fusion | bytes 4194308 | tf_op jit(solution)/shard_map/while/body/eval_jaxpr/dynamic_slice | solution.py:48
  239.8 11.8 %conditional.4 = (f32[1,16,256]{2,1,0:T(8,128)}, f32[1,16,256]{2,1,0:T(8,128)S(1)}, f32[1,16,256,64]{2,3,1,0:T(8,128)}) conditional(s32[]{:T(128)} %bitcast.87, (f32[16,256]{1,0:T(8,128)}, f32[16,256]{1,0:T(8,128)S(1)}, f32[16,256,64]{1,2,0:T(8,128)}) %tuple.129, (s32[512]{0:T(512)S(1)}, s32[256]{0:T(256)S(1)}, bf16[2,256,16,64]{1,3,2,0:T(8,128)(2,1)}, ...), branch_computations={%region_8.8_spmd, %region_9.0_spmd} | conditional | flops 564797440 | bytes 43224172 | solution.py:70
  240.0 2.9 %fusion.18 = (f32[16,256]{1,0:T(8,128)S(1)}, f32[16,256,512]{2,1,0:T(8,128)S(1)}) fusion(pred[256,512]{1,0:T(8,128)(4,1)S(1)} %broadcast_compare_fusion.1, bf16[512,16,64]{0,2,1:T(8,128)(2,1)S(1)} %get-tuple-element.254, bf16[2,256,16,64]{1,3,2,0:T(8,128)(2,1)} %get-tuple-element.253), kind=kOutput, calls=%fused_computation.20 | convolution fusion | flops 274722816 | bytes 10108928 | tf_op jit(solution)/shard_map/while/body/eval_jaxpr/cond/branch_1_fun/rhd,khd->hrk/dot_general | solution.py:21
  243.5 3.2 %fusion.20 = f32[16,256]{1,0:T(8,128)S(1)} fusion(f32[16,256,512]{2,1,0:T(8,128)S(1)} %get-tuple-element.368, f32[16,256]{1,0:T(8,128)} %max.5, pred[256,512]{1,0:T(8,128)(4,1)S(1)} %broadcast_compare_fusion.1), kind=kLoop, calls=%fused_computation.22 | loop fusion | flops 10481664 | bytes 8552448 | tf_op jit(solution)/shard_map/while/body/eval_jaxpr/cond/branch_1_fun/reduce_sum | solution.py:29
  247.5 3.1 %fusion.27 = f32[1,16,256,64]{2,3,1,0:T(8,128)S(1)} fusion(bf16[512,16,64]{0,2,1:T(8,128)(2,1)S(1)} %copy-done.5, f32[16,256,512]{2,1,0:T(8,128)S(1)} %get-tuple-element.368, f32[16,256]{1,0:T(8,128)} %max.5, pred[256,512]{1,0:T(8,128)(4,1)S(1)} %broadcast_compare_fusion.1, f32[16,256,64]{1,2,0:T(8,128)S(1)} %copy-done.3, f32[16,256]{1,0:T(8,128)S(1)} %get-tuple-element.364), kind=kOutput, calls=%fused_computation.26 | convolution fusion | flops 279445504 | bytes 11698176 | tf_op jit(solution)/shard_map/while/body/eval_jaxpr/cond/branch_1_fun/hrk,khd->hrd/dot_general | solution.py:30
  254.3 11.8 %conditional.5 = (f32[1,16,256]{2,1,0:T(8,128)}, f32[1,16,256]{2,1,0:T(8,128)S(1)}, f32[1,16,256,64]{2,3,1,0:T(8,128)}) conditional(s32[]{:T(128)} %bitcast.90, (f32[16,256]{1,0:T(8,128)}, f32[16,256]{1,0:T(8,128)S(1)}, f32[16,256,64]{1,2,0:T(8,128)}) %tuple.131, (s32[512]{0:T(512)S(1)}, s32[256]{0:T(256)S(1)}, bf16[2,256,16,64]{1,3,2,0:T(8,128)(2,1)}, ...), branch_computations={%region_4.4_spmd, %region_5.0_spmd} | conditional | flops 564797440 | bytes 43224172 | solution.py:70
  258.0 3.2 %fusion.2 = f32[16,256]{1,0:T(8,128)S(1)} fusion(f32[16,256,512]{2,1,0:T(8,128)S(1)} %get-tuple-element.366, f32[16,256]{1,0:T(8,128)} %max.4, pred[256,512]{1,0:T(8,128)(4,1)S(1)} %broadcast_compare_fusion), kind=kLoop, calls=%fused_computation.4 | loop fusion | flops 10481664 | bytes 8552448 | tf_op jit(solution)/shard_map/while/body/eval_jaxpr/cond/branch_1_fun/reduce_sum | solution.py:29
  262.0 3.1 %fusion.9 = f32[1,16,256,64]{2,3,1,0:T(8,128)S(1)} fusion(bf16[512,16,64]{0,2,1:T(8,128)(2,1)S(1)} %copy-done.6, f32[16,256,512]{2,1,0:T(8,128)S(1)} %get-tuple-element.366, f32[16,256]{1,0:T(8,128)} %max.4, pred[256,512]{1,0:T(8,128)(4,1)S(1)} %broadcast_compare_fusion, f32[16,256,64]{1,2,0:T(8,128)S(1)} %copy-done.1, f32[16,256]{1,0:T(8,128)S(1)} %get-tuple-element.362), kind=kOutput, calls=%fused_computation.8 | convolution fusion | flops 279445504 | bytes 11698176 | tf_op jit(solution)/shard_map/while/body/eval_jaxpr/cond/branch_1_fun/hrk,khd->hrd/dot_general | solution.py:30
  266.9 3.1 %pad_maximum_fusion.8 = f32[2,16,256,64]{2,3,1,0:T(8,128)} fusion(f32[1,16,256,64]{2,3,1,0:T(8,128)} %get-tuple-element.472, f32[1,16,256,64]{2,3,1,0:T(8,128)} %get-tuple-element.473), kind=kLoop, calls=%fused_computation.36.clone.1 | loop fusion | flops 524288 | bytes 4194304 | tf_op jit(solution)/shard_map/while/body/eval_jaxpr/stack | solution.py:71
  (101 shorter events, 56.0 us)
Async XLA Ops:
  6.5 266.6 %copy-start = (bf16[1024,1024]{1,0:T(8,128)(2,1)S(1)}, bf16[1024,1024]{1,0:T(8,128)(2,1)}, u32[]{:S(2)}) copy-start(bf16[1024,1024]{1,0:T(8,128)(2,1)} %param.24) | copy-start | bytes 6291460
  6.5 37.3 %copy-start.10 = (bf16[1024]{0:T(1024)(128)(2,1)S(1)}, bf16[1024]{0:T(1024)(128)(2,1)}, u32[]{:S(2)}) copy-start(bf16[1024]{0:T(1024)(128)(2,1)} %param.20) | copy-start | bytes 6148
  37.7 28.5 %all-to-all-start.1 = ((bf16[8,2,32768]{2,1,0:T(2,128)(2,1)}), bf16[8,2,32768]{2,1,0:T(2,128)(2,1)S(1)}, u32[]{:S(2)}, u32[]{:S(2)}) async-start(bf16[8,2,32768]{2,1,0:T(2,128)(2,1)} %reshape.138), calls=%async_computation.1 | async-start | bytes 2097152 | tf_op jit(solution)/shard_map/all_to_all | solution.py:93
  43.9 86.8 %all-gather.3.cloned.1.call-start = ((), (), s32[]{:S(2)}) async-start(), calls=%async_computation.2 | async-start | bytes 2359296 | tf_op jit(solution)/shard_map/all_gather | solution.py:125
  74.0 5.7 %copy-start.8 = (bf16[1024,1024]{1,0:T(8,128)(2,1)S(1)}, bf16[1024,1024]{1,0:T(8,128)(2,1)}, u32[]{:S(2)}) copy-start(bf16[1024,1024]{1,0:T(8,128)(2,1)} %param.22) | copy-start | bytes 6291460
  74.0 10.1 %copy-start.9 = (s32[1,1024]{1,0:T(1,128)S(1)}, s32[1,1024]{1,0:T(1,128)}, u32[]{:S(2)}) copy-start(s32[1,1024]{1,0:T(1,128)} %param.18) | copy-start | bytes 12292
  78.9 0.8 copy-start.7
  80.9 12.7 %copy-start.11 = (bf16[1024]{0:T(1024)(128)(2,1)S(1)}, bf16[1024]{0:T(1024)(128)(2,1)}, u32[]{:S(2)}) copy-start(bf16[1024]{0:T(1024)(128)(2,1)} %param.25) | copy-start | bytes 6148
  80.9 99.5 %all-gather.5.cloned.1.call-start = ((), (), s32[]{:S(2)}) async-start(), calls=%async_computation.3 | async-start | bytes 2359296 | tf_op jit(solution)/shard_map/all_gather | solution.py:126
  195.9 7.5 %copy-start.3 = (f32[16,256,64]{1,2,0:T(8,128)S(1)}, f32[16,256,64]{1,2,0:T(8,128)}, u32[]{:S(2)}) copy-start(f32[16,256,64]{1,2,0:T(8,128)} %get-tuple-element.256) | copy-start | bytes 3145732 | tf_op jit(solution)/shard_map/while/body/eval_jaxpr/cond
  196.0 7.5 %copy-start.5 = (bf16[512,16,64]{0,2,1:T(8,128)(2,1)S(1)}, bf16[512,16,64]{0,2,1:T(8,128)(2,1)}, u32[]{:S(2)}) copy-start(bf16[512,16,64]{0,2,1:T(8,128)(2,1)} %get-tuple-element.257) | copy-start | bytes 3145732 | tf_op jit(solution)/shard_map/while/body/eval_jaxpr/cond
  206.6 1.0 copy-start.4
  210.5 7.5 %copy-start.1 = (f32[16,256,64]{1,2,0:T(8,128)S(1)}, f32[16,256,64]{1,2,0:T(8,128)}, u32[]{:S(2)}) copy-start(f32[16,256,64]{1,2,0:T(8,128)} %get-tuple-element.248) | copy-start | bytes 3145732 | tf_op jit(solution)/shard_map/while/body/eval_jaxpr/cond
  210.5 7.5 %copy-start.6 = (bf16[512,16,64]{0,2,1:T(8,128)(2,1)S(1)}, bf16[512,16,64]{0,2,1:T(8,128)(2,1)}, u32[]{:S(2)}) copy-start(bf16[512,16,64]{0,2,1:T(8,128)(2,1)} %get-tuple-element.249) | copy-start | bytes 3145732 | tf_op jit(solution)/shard_map/while/body/eval_jaxpr/cond
  221.2 1.0 copy-start.2
  240.0 7.5 %copy-start.3 = (f32[16,256,64]{1,2,0:T(8,128)S(1)}, f32[16,256,64]{1,2,0:T(8,128)}, u32[]{:S(2)}) copy-start(f32[16,256,64]{1,2,0:T(8,128)} %get-tuple-element.256) | copy-start | bytes 3145732 | tf_op jit(solution)/shard_map/while/body/eval_jaxpr/cond
  240.0 7.5 %copy-start.5 = (bf16[512,16,64]{0,2,1:T(8,128)(2,1)S(1)}, bf16[512,16,64]{0,2,1:T(8,128)(2,1)}, u32[]{:S(2)}) copy-start(bf16[512,16,64]{0,2,1:T(8,128)(2,1)} %get-tuple-element.257) | copy-start | bytes 3145732 | tf_op jit(solution)/shard_map/while/body/eval_jaxpr/cond
  250.7 1.0 copy-start.4
  254.5 7.5 %copy-start.1 = (f32[16,256,64]{1,2,0:T(8,128)S(1)}, f32[16,256,64]{1,2,0:T(8,128)}, u32[]{:S(2)}) copy-start(f32[16,256,64]{1,2,0:T(8,128)} %get-tuple-element.248) | copy-start | bytes 3145732 | tf_op jit(solution)/shard_map/while/body/eval_jaxpr/cond
  254.5 7.5 %copy-start.6 = (bf16[512,16,64]{0,2,1:T(8,128)(2,1)S(1)}, bf16[512,16,64]{0,2,1:T(8,128)(2,1)}, u32[]{:S(2)}) copy-start(bf16[512,16,64]{0,2,1:T(8,128)(2,1)} %get-tuple-element.249) | copy-start | bytes 3145732 | tf_op jit(solution)/shard_map/while/body/eval_jaxpr/cond
  265.2 1.0 copy-start.2
Sparse Core Ops, SparseCore 0:
  81.1 49.5 all-gather.2
  132.7 47.6 all-gather.4
where the time goes:
time: 286 us; the launch traced here: 284 us
  waiting for transfers between devices  109 us (38%)
  local copies, waits for them, and re-layouts  54.5 us (19%)
  matrix products  39.1 us (14%)
  other arithmetic  38 us (13%)
  blocking collectives  18 us (6%)
  between operations  13.5 us (5%)
  starting transfers between devices  6.39 us (2%)
  loops' own time  5.51 us (2%)
    all_gather x1, waiting for transfers between devices, per_device(): lax.all_gather(value_rows, 'mp', axis=0, tiled=True)  49.8 us
    all_gather x1, waiting for transfers between devices, per_device(): lax.all_gather(key_rows, 'mp', axis=0, tiled=True)  36.8 us
    all_to_all x1, waiting for transfers between devices, per_device(): lax.all_to_all(lax.all_to_all(patch_latents, 'seq', split_axis=0, concat_...  22.3 us
    all_to_all x1, blocking collectives, per_device(): lax.all_to_all(patch_latents, 'seq', split_axis=0, concat_axis=1, tiled=T...  18 us
    reduce_sum x4, other arithmetic, fold_block(): denominator = denominator * correction + jnp.sum(raised, axis=-1)  12.9 us
    dot_general x4, matrix products, fold_block(): jnp.einsum('hrk,khd->hrd', raised.astype(jnp.bfloat16), value_block, pref...  12.6 us
    dot_general x4, matrix products, fold_block(): jnp.einsum('rhd,khd->hrk', query_part, key_block, preferred_element_type=...  11.7 us
    another operation x10, other arithmetic, one_block(): jnp.stack([updated[0][slot], updated[1][slot]])  10.6 us
  transfers between devices with their start and end apart: 3, of which 3 were waited for; matrix products, arithmetic and copies ran while one was open for 4% of the time, Pallas kernels for 0%

commit v1 on v0

--- a/solution.py
+++ b/solution.py
@@ -91,7 +91,12 @@
     tokens_here = byte_states.shape[1]
     half_rows = tokens_here // 2
     regrouped = lax.all_to_all(
-        lax.all_to_all(patch_latents, "seq", split_axis=0, concat_axis=1, tiled=True),
+        jnp.concatenate(
+            lax.all_to_all(
+                jnp.stack(jnp.split(patch_latents, lax.axis_size("seq"), axis=0)), "seq", 0, 0
+            ),
+            axis=1,
+        ),
         "mp",
         split_axis=1,
         concat_axis=2,

time: 286 us -> 286 us (level)
    all_to_all x2 -> x1, local copies, waits for them, and re-layouts: 4.58 us -> 1.61 us  [per_device(): lax.all_to_all(jnp.concatenate(lax.all_to_all(jnp.stack(jnp.split(patch_l...]
    reshape x0 -> x1, local copies, waits for them, and re-layouts: none -> 2.96 us  [per_device(): jnp.concatenate(lax.all_to_all(jnp.stack(jnp.split(patch_latents, lax.axi...]
where the time goes in v1:
time: 286 us; the launch traced here: 284 us
  waiting for transfers between devices  109 us (38%)
  local copies, waits for them, and re-layouts  55.7 us (19%)
  matrix products  39.1 us (14%)
  other arithmetic  38.1 us (13%)
  blocking collectives  17 us (6%)
  between operations  13.5 us (5%)
  starting transfers between devices  6.39 us (2%)
  loops' own time  5.07 us (2%)
    all_gather x1, waiting for transfers between devices, per_device(): lax.all_gather(value_rows, 'mp', axis=0, tiled=True)  49.8 us
    all_gather x1, waiting for transfers between devices, per_device(): lax.all_gather(key_rows, 'mp', axis=0, tiled=True)  36.8 us
    all_to_all x1, waiting for transfers between devices, per_device(): lax.all_to_all(jnp.concatenate(lax.all_to_all(jnp.stack(jnp.split(patch_l...  22.3 us
    all_to_all x1, blocking collectives, per_device(): lax.all_to_all(jnp.stack(jnp.split(patch_latents, lax.axis_size('seq'), a...  17 us
    reduce_sum x4, other arithmetic, fold_block(): denominator = denominator * correction + jnp.sum(raised, axis=-1)  12.9 us
    dot_general x4, matrix products, fold_block(): jnp.einsum('hrk,khd->hrd', raised.astype(jnp.bfloat16), value_block, pref...  12.6 us
    dot_general x4, matrix products, fold_block(): jnp.einsum('rhd,khd->hrk', query_part, key_block, preferred_element_type=...  11.7 us
    another operation x10, other arithmetic, one_block(): jnp.stack([updated[0][slot], updated[1][slot]])  10.6 us
  transfers between devices with their start and end apart: 3, of which 3 were waited for; matrix products, arithmetic and copies ran while one was open for 4% of the time, Pallas kernels for 0%

profile of v1, /device:TPU:16, one launch (start us, length us, event | category | flops | bytes accessed | tf_op | source)
XLA Modules:
  0.0 283.8 jit_solution(10535084629590974657)
XLA Ops:
  8.1 17.0 %all_to_all.20 = bf16[4,1,256,512]{3,2,1,0:T(8,128)(2,1)S(1)} all-to-all(bf16[4,1,256,512]{3,2,1,0:T(8,128)(2,1)S(1)} %pad_maximum_fusion.3), channel_id=1, replica_groups=mesh['seq'=4,'mp'=8] {'seq'}, dimensions={0} | all-to-all | bytes 2097152 | tf_op jit(solution)/shard_map/all_to_all | solution.py:95
  25.1 3.0 %copy.52 = bf16[1,1024,512]{2,0,1:T(2,128)(2,1)} copy(bf16[1,1024,512]{2,1,0:T(8,128)(2,1)S(1)} %bitcast.108) | data formatting | bytes 2097152 | tf_op jit(solution)/shard_map/reshape | solution.py:94
  28.6 8.0 %reduce.2 = bf16[1024,512]{1,0:T(8,128)(2,1)S(1)} reduce(bf16[1024,1,512]{2,1,0:T(2,128)(2,1)} %bitcast.106, bf16[]{:T(256)} %broadcast.104), dimensions={1}, to_apply=%bitcast.86.reduce_sub_computation | reduce | bytes 2097154
  38.2 6.2 %all-to-all-start.1 = ((bf16[8,2,32768]{2,1,0:T(2,128)(2,1)}), bf16[8,2,32768]{2,1,0:T(2,128)(2,1)S(1)}, u32[]{:S(2)}, u32[]{:S(2)}) async-start(bf16[8,2,32768]{2,1,0:T(2,128)(2,1)} %reshape.139), calls=%async_computation.1 | async-start | bytes 2097152 | tf_op jit(solution)/shard_map/all_to_all | solution.py:93
  44.4 22.3 %all-to-all-done.1 = bf16[8,2,32768]{2,1,0:T(2,128)(2,1)S(1)} async-done(((bf16[8,2,32768]{2,1,0:T(2,128)(2,1)}), bf16[8,2,32768]{2,1,0:T(2,128)(2,1)S(1)}, u32[]{:S(2)}, u32[]{:S(2)}) %all-to-all-start.1) | async-done | bytes 1048608 | tf_op jit(solution)/shard_map/all_to_all | solution.py:93
  66.6 3.4 %reshape.140 = bf16[1024,1,512]{2,1,0:T(2,128)(2,1)} reshape(bf16[8,2,32768]{2,1,0:T(2,128)(2,1)S(1)} %all-to-all-done.1) | data formatting | bytes 2097152
  74.6 4.9 %multiply_reduce_fusion.1 = (f32[128]{0:T(128)S(1)}, f32[128,1024]{1,0:T(8,128)S(1)}) fusion(bf16[128,4096]{0,1:T(8,128)(2,1)S(1)} %bitcast.107, bf16[4096,1024]{1,0:T(8,128)(2,1)} %param.19), kind=kOutput, calls=%fused_computation.59 | convolution fusion | flops 1074003840 | bytes 9961984 | tf_op jit(solution)/shard_map/dot_general | solution.py:105
  81.7 3.0 %convolution_convert_fusion.1 = bf16[128,1024]{1,0:T(8,128)(2,1)} fusion(bf16[1024,1024]{1,0:T(8,128)(2,1)} %param.23, f32[128,1024]{1,0:T(8,128)} %copy-done.7, f32[1024]{0:T(1024)S(1)} %convert_element_type.60, f32[128]{0:T(128)S(1)} %add_rsqrt_fusion.1), kind=kOutput, calls=%fused_computation.52 | convolution fusion | flops 268959744 | bytes 2888192 | tf_op jit(solution)/shard_map/dot_general | solution.py:123
  85.1 3.2 %convolution_convert_fusion = bf16[512,1024]{1,0:T(8,128)(2,1)S(1)} fusion(bf16[1024,1024]{1,0:T(8,128)(2,1)} %param.21, bf16[1,512,1024]{2,1,0:T(8,128)(2,1)} %param.16), kind=kOutput, calls=%fused_computation.51 | convolution fusion | flops 1074266112 | bytes 4194304 | tf_op jit(solution)/shard_map/dot_general | solution.py:115
  90.6 3.6 %copy.43 = bf16[2,256,16,64]{1,3,2,0:T(8,128)(2,1)} copy(bf16[2,256,16,64]{3,2,1,0:T(8,128)(2,1)} %reshape.137) | data formatting | bytes 2097152 | tf_op jit(solution)/shard_map/while | solution.py:73
  94.4 36.8 %all-gather.3.cloned.1.call-done = bf16[1024,1024]{1,0:T(8,128)(2,1)} async-done(((bf16[128,1024]{1,0:T(8,128)(2,1)}), bf16[1024,1024]{1,0:T(8,128)(2,1)}) %all-gather.3.cloned.1.call-update) | async-done | bytes 2097168 | tf_op jit(solution)/shard_map/all_gather | solution.py:130
  131.2 49.8 %all-gather.5.cloned.1.call-done = bf16[1024,1024]{1,0:T(8,128)(2,1)} async-done(((bf16[128,1024]{1,0:T(8,128)(2,1)}), bf16[1024,1024]{1,0:T(8,128)(2,1)}) %all-gather.5.cloned.1.call-update) | async-done | bytes 2097168 | tf_op jit(solution)/shard_map/all_gather | solution.py:131
  182.5 87.3 %while.17 = (s32[]{:T(128)}, f32[2,16,256]{2,1,0:T(8,128)S(1)}, f32[2,16,256]{2,1,0:T(8,128)S(1)}, f32[2,16,256,64]{2,3,1,0:T(8,128)}, s32[1024]{0:T(1024)S(1)},...) while((s32[]{:T(128)}, f32[2,16,256]{2,1,0:T(8,128)S(1)}, ...), condition=%wide.region_12.13_spmd, body=%wide.region_3.12_spmd.sunk | while | flops 1130135552 | bytes 103557752 | solution.py:73
  185.6 3.1 %slice_bitcast_fusion.13 = (f32[16,256,64]{1,2,0:T(8,128)}, f32[16,256,64]{1,2,0:T(8,128)}) fusion(f32[2,16,256,64]{2,3,1,0:T(8,128)} %get-tuple-element.517), kind=kLoop, calls=%fused_computation.38.clone.1 | loop fusion | bytes 4194304 | tf_op jit(solution)/shard_map/while/body/eval_jaxpr/squeeze | solution.py:54
  188.7 3.0 %constant_dynamic-slice_fusion.3 = (bf16[512,1024]{1,0:T(8,128)(2,1)}, bf16[512,1024]{1,0:T(8,128)(2,1)}) fusion(bf16[1024,1024]{1,0:T(8,128)(2,1)} %get-tuple-element.535, s32[]{:T(128)S(6)} %select_n.71, bf16[1024,1024]{1,0:T(8,128)(2,1)} %get-tuple-element.534), kind=kLoop, calls=%fused_computation.45.clone.1 | loop fusion | bytes 4194308 | tf_op jit(solution)/shard_map/while/body/eval_jaxpr/dynamic_slice | solution.py:48
  196.2 11.9 %conditional.4 = (f32[1,16,256]{2,1,0:T(8,128)}, f32[1,16,256]{2,1,0:T(8,128)S(1)}, f32[1,16,256,64]{2,3,1,0:T(8,128)}) conditional(s32[]{:T(128)} %bitcast.95, (f32[16,256]{1,0:T(8,128)}, f32[16,256]{1,0:T(8,128)S(1)}, f32[16,256,64]{1,2,0:T(8,128)}) %tuple.133, (s32[512]{0:T(512)S(1)}, s32[256]{0:T(256)S(1)}, bf16[2,256,16,64]{1,3,2,0:T(8,128)(2,1)}, ...), branch_computations={%region_8.8_spmd, %region_9.0_spmd} | conditional | flops 564797440 | bytes 43224172 | solution.py:70
  196.4 2.9 %fusion.18 = (f32[16,256]{1,0:T(8,128)S(1)}, f32[16,256,512]{2,1,0:T(8,128)S(1)}) fusion(pred[256,512]{1,0:T(8,128)(4,1)S(1)} %broadcast_compare_fusion.1, bf16[512,16,64]{0,2,1:T(8,128)(2,1)S(1)} %get-tuple-element.254, bf16[2,256,16,64]{1,3,2,0:T(8,128)(2,1)} %get-tuple-element.253), kind=kOutput, calls=%fused_computation.20 | convolution fusion | flops 274722816 | bytes 10108928 | tf_op jit(solution)/shard_map/while/body/eval_jaxpr/cond/branch_1_fun/rhd,khd->hrk/dot_general | solution.py:21
  199.9 3.2 %fusion.20 = f32[16,256]{1,0:T(8,128)S(1)} fusion(f32[16,256,512]{2,1,0:T(8,128)S(1)} %get-tuple-element.378, f32[16,256]{1,0:T(8,128)} %max.5, pred[256,512]{1,0:T(8,128)(4,1)S(1)} %broadcast_compare_fusion.1), kind=kLoop, calls=%fused_computation.22 | loop fusion | flops 10481664 | bytes 8552448 | tf_op jit(solution)/shard_map/while/body/eval_jaxpr/cond/branch_1_fun/reduce_sum | solution.py:29
  203.9 3.2 %fusion.27 = f32[1,16,256,64]{2,3,1,0:T(8,128)S(1)} fusion(bf16[512,16,64]{0,2,1:T(8,128)(2,1)S(1)} %copy-done.5, f32[16,256,512]{2,1,0:T(8,128)S(1)} %get-tuple-element.378, f32[16,256]{1,0:T(8,128)} %max.5, pred[256,512]{1,0:T(8,128)(4,1)S(1)} %broadcast_compare_fusion.1, f32[16,256,64]{1,2,0:T(8,128)S(1)} %copy-done.3, f32[16,256]{1,0:T(8,128)S(1)} %get-tuple-element.374), kind=kOutput, calls=%fused_computation.26 | convolution fusion | flops 279445504 | bytes 11698176 | tf_op jit(solution)/shard_map/while/body/eval_jaxpr/cond/branch_1_fun/hrk,khd->hrd/dot_general | solution.py:30
  210.5 11.8 %conditional.5 = (f32[1,16,256]{2,1,0:T(8,128)}, f32[1,16,256]{2,1,0:T(8,128)S(1)}, f32[1,16,256,64]{2,3,1,0:T(8,128)}) conditional(s32[]{:T(128)} %bitcast.98, (f32[16,256]{1,0:T(8,128)}, f32[16,256]{1,0:T(8,128)S(1)}, f32[16,256,64]{1,2,0:T(8,128)}) %tuple.135, (s32[512]{0:T(512)S(1)}, s32[256]{0:T(256)S(1)}, bf16[2,256,16,64]{1,3,2,0:T(8,128)(2,1)}, ...), branch_computations={%region_4.4_spmd, %region_5.0_spmd} | conditional | flops 564797440 | bytes 43224172 | solution.py:70
  214.2 3.2 %fusion.2 = f32[16,256]{1,0:T(8,128)S(1)} fusion(f32[16,256,512]{2,1,0:T(8,128)S(1)} %get-tuple-element.376, f32[16,256]{1,0:T(8,128)} %max.4, pred[256,512]{1,0:T(8,128)(4,1)S(1)} %broadcast_compare_fusion), kind=kLoop, calls=%fused_computation.4 | loop fusion | flops 10481664 | bytes 8552448 | tf_op jit(solution)/shard_map/while/body/eval_jaxpr/cond/branch_1_fun/reduce_sum | solution.py:29
  218.2 3.2 %fusion.9 = f32[1,16,256,64]{2,3,1,0:T(8,128)S(1)} fusion(bf16[512,16,64]{0,2,1:T(8,128)(2,1)S(1)} %copy-done.6, f32[16,256,512]{2,1,0:T(8,128)S(1)} %get-tuple-element.376, f32[16,256]{1,0:T(8,128)} %max.4, pred[256,512]{1,0:T(8,128)(4,1)S(1)} %broadcast_compare_fusion, f32[16,256,64]{1,2,0:T(8,128)S(1)} %copy-done.1, f32[16,256]{1,0:T(8,128)S(1)} %get-tuple-element.372), kind=kOutput, calls=%fused_computation.8 | convolution fusion | flops 279445504 | bytes 11698176 | tf_op jit(solution)/shard_map/while/body/eval_jaxpr/cond/branch_1_fun/hrk,khd->hrd/dot_general | solution.py:30
  223.1 3.1 %pad_maximum_fusion.9 = f32[2,16,256,64]{2,3,1,0:T(8,128)} fusion(f32[1,16,256,64]{2,3,1,0:T(8,128)} %get-tuple-element.486, f32[1,16,256,64]{2,3,1,0:T(8,128)} %get-tuple-element.487), kind=kLoop, calls=%fused_computation.36.clone.1 | loop fusion | flops 524288 | bytes 4194304 | tf_op jit(solution)/shard_map/while/body/eval_jaxpr/stack | solution.py:71
  229.2 3.1 %slice_bitcast_fusion.13 = (f32[16,256,64]{1,2,0:T(8,128)}, f32[16,256,64]{1,2,0:T(8,128)}) fusion(f32[2,16,256,64]{2,3,1,0:T(8,128)} %get-tuple-element.517), kind=kLoop, calls=%fused_computation.38.clone.1 | loop fusion | bytes 4194304 | tf_op jit(solution)/shard_map/while/body/eval_jaxpr/squeeze | solution.py:54
  232.4 3.0 %constant_dynamic-slice_fusion.3 = (bf16[512,1024]{1,0:T(8,128)(2,1)}, bf16[512,1024]{1,0:T(8,128)(2,1)}) fusion(bf16[1024,1024]{1,0:T(8,128)(2,1)} %get-tuple-element.535, s32[]{:T(128)S(6)} %select_n.71, bf16[1024,1024]{1,0:T(8,128)(2,1)} %get-tuple-element.534), kind=kLoop, calls=%fused_computation.45.clone.1 | loop fusion | bytes 4194308 | tf_op jit(solution)/shard_map/while/body/eval_jaxpr/dynamic_slice | solution.py:48
  239.9 11.9 %conditional.4 = (f32[1,16,256]{2,1,0:T(8,128)}, f32[1,16,256]{2,1,0:T(8,128)S(1)}, f32[1,16,256,64]{2,3,1,0:T(8,128)}) conditional(s32[]{:T(128)} %bitcast.95, (f32[16,256]{1,0:T(8,128)}, f32[16,256]{1,0:T(8,128)S(1)}, f32[16,256,64]{1,2,0:T(8,128)}) %tuple.133, (s32[512]{0:T(512)S(1)}, s32[256]{0:T(256)S(1)}, bf16[2,256,16,64]{1,3,2,0:T(8,128)(2,1)}, ...), branch_computations={%region_8.8_spmd, %region_9.0_spmd} | conditional | flops 564797440 | bytes 43224172 | solution.py:70
  243.6 3.2 %fusion.20 = f32[16,256]{1,0:T(8,128)S(1)} fusion(f32[16,256,512]{2,1,0:T(8,128)S(1)} %get-tuple-element.378, f32[16,256]{1,0:T(8,128)} %max.5, pred[256,512]{1,0:T(8,128)(4,1)S(1)} %broadcast_compare_fusion.1), kind=kLoop, calls=%fused_computation.22 | loop fusion | flops 10481664 | bytes 8552448 | tf_op jit(solution)/shard_map/while/body/eval_jaxpr/cond/branch_1_fun/reduce_sum | solution.py:29
  247.5 3.1 %fusion.27 = f32[1,16,256,64]{2,3,1,0:T(8,128)S(1)} fusion(bf16[512,16,64]{0,2,1:T(8,128)(2,1)S(1)} %copy-done.5, f32[16,256,512]{2,1,0:T(8,128)S(1)} %get-tuple-element.378, f32[16,256]{1,0:T(8,128)} %max.5, pred[256,512]{1,0:T(8,128)(4,1)S(1)} %broadcast_compare_fusion.1, f32[16,256,64]{1,2,0:T(8,128)S(1)} %copy-done.3, f32[16,256]{1,0:T(8,128)S(1)} %get-tuple-element.374), kind=kOutput, calls=%fused_computation.26 | convolution fusion | flops 279445504 | bytes 11698176 | tf_op jit(solution)/shard_map/while/body/eval_jaxpr/cond/branch_1_fun/hrk,khd->hrd/dot_general | solution.py:30
  254.2 11.8 %conditional.5 = (f32[1,16,256]{2,1,0:T(8,128)}, f32[1,16,256]{2,1,0:T(8,128)S(1)}, f32[1,16,256,64]{2,3,1,0:T(8,128)}) conditional(s32[]{:T(128)} %bitcast.98, (f32[16,256]{1,0:T(8,128)}, f32[16,256]{1,0:T(8,128)S(1)}, f32[16,256,64]{1,2,0:T(8,128)}) %tuple.135, (s32[512]{0:T(512)S(1)}, s32[256]{0:T(256)S(1)}, bf16[2,256,16,64]{1,3,2,0:T(8,128)(2,1)}, ...), branch_computations={%region_4.4_spmd, %region_5.0_spmd} | conditional | flops 564797440 | bytes 43224172 | solution.py:70
  257.9 3.2 %fusion.2 = f32[16,256]{1,0:T(8,128)S(1)} fusion(f32[16,256,512]{2,1,0:T(8,128)S(1)} %get-tuple-element.376, f32[16,256]{1,0:T(8,128)} %max.4, pred[256,512]{1,0:T(8,128)(4,1)S(1)} %broadcast_compare_fusion), kind=kLoop, calls=%fused_computation.4 | loop fusion | flops 10481664 | bytes 8552448 | tf_op jit(solution)/shard_map/while/body/eval_jaxpr/cond/branch_1_fun/reduce_sum | solution.py:29
  261.9 3.2 %fusion.9 = f32[1,16,256,64]{2,3,1,0:T(8,128)S(1)} fusion(bf16[512,16,64]{0,2,1:T(8,128)(2,1)S(1)} %copy-done.6, f32[16,256,512]{2,1,0:T(8,128)S(1)} %get-tuple-element.376, f32[16,256]{1,0:T(8,128)} %max.4, pred[256,512]{1,0:T(8,128)(4,1)S(1)} %broadcast_compare_fusion, f32[16,256,64]{1,2,0:T(8,128)S(1)} %copy-done.1, f32[16,256]{1,0:T(8,128)S(1)} %get-tuple-element.372), kind=kOutput, calls=%fused_computation.8 | convolution fusion | flops 279445504 | bytes 11698176 | tf_op jit(solution)/shard_map/while/body/eval_jaxpr/cond/branch_1_fun/hrk,khd->hrd/dot_general | solution.py:30
  266.8 3.1 %pad_maximum_fusion.9 = f32[2,16,256,64]{2,3,1,0:T(8,128)} fusion(f32[1,16,256,64]{2,3,1,0:T(8,128)} %get-tuple-element.486, f32[1,16,256,64]{2,3,1,0:T(8,128)} %get-tuple-element.487), kind=kLoop, calls=%fused_computation.36.clone.1 | loop fusion | flops 524288 | bytes 4194304 | tf_op jit(solution)/shard_map/while/body/eval_jaxpr/stack | solution.py:71
  (103 shorter events, 57.3 us)
Async XLA Ops:
  6.5 266.5 %copy-start = (bf16[1024,1024]{1,0:T(8,128)(2,1)S(1)}, bf16[1024,1024]{1,0:T(8,128)(2,1)}, u32[]{:S(2)}) copy-start(bf16[1024,1024]{1,0:T(8,128)(2,1)} %param.24) | copy-start | bytes 6291460
  6.5 37.8 %copy-start.10 = (bf16[1024]{0:T(1024)(128)(2,1)S(1)}, bf16[1024]{0:T(1024)(128)(2,1)}, u32[]{:S(2)}) copy-start(bf16[1024]{0:T(1024)(128)(2,1)} %param.20) | copy-start | bytes 6148
  38.2 28.5 %all-to-all-start.1 = ((bf16[8,2,32768]{2,1,0:T(2,128)(2,1)}), bf16[8,2,32768]{2,1,0:T(2,128)(2,1)S(1)}, u32[]{:S(2)}, u32[]{:S(2)}) async-start(bf16[8,2,32768]{2,1,0:T(2,128)(2,1)} %reshape.139), calls=%async_computation.1 | async-start | bytes 2097152 | tf_op jit(solution)/shard_map/all_to_all | solution.py:93
  44.4 86.8 %all-gather.3.cloned.1.call-start = ((), (), s32[]{:S(2)}) async-start(), calls=%async_computation.2 | async-start | bytes 2359296 | tf_op jit(solution)/shard_map/all_gather | solution.py:130
  74.6 5.7 %copy-start.8 = (bf16[1024,1024]{1,0:T(8,128)(2,1)S(1)}, bf16[1024,1024]{1,0:T(8,128)(2,1)}, u32[]{:S(2)}) copy-start(bf16[1024,1024]{1,0:T(8,128)(2,1)} %param.22) | copy-start | bytes 6291460
  74.6 10.1 %copy-start.9 = (s32[1,1024]{1,0:T(1,128)S(1)}, s32[1,1024]{1,0:T(1,128)}, u32[]{:S(2)}) copy-start(s32[1,1024]{1,0:T(1,128)} %param.18) | copy-start | bytes 12292
  79.5 0.8 copy-start.7
  81.5 12.7 %copy-start.11 = (bf16[1024]{0:T(1024)(128)(2,1)S(1)}, bf16[1024]{0:T(1024)(128)(2,1)}, u32[]{:S(2)}) copy-start(bf16[1024]{0:T(1024)(128)(2,1)} %param.25) | copy-start | bytes 6148
  81.5 99.5 %all-gather.5.cloned.1.call-start = ((), (), s32[]{:S(2)}) async-start(), calls=%async_computation.3 | async-start | bytes 2359296 | tf_op jit(solution)/shard_map/all_gather | solution.py:131
  196.3 7.5 %copy-start.3 = (f32[16,256,64]{1,2,0:T(8,128)S(1)}, f32[16,256,64]{1,2,0:T(8,128)}, u32[]{:S(2)}) copy-start(f32[16,256,64]{1,2,0:T(8,128)} %get-tuple-element.256) | copy-start | bytes 3145732 | tf_op jit(solution)/shard_map/while/body/eval_jaxpr/cond
  196.3 7.5 %copy-start.5 = (bf16[512,16,64]{0,2,1:T(8,128)(2,1)S(1)}, bf16[512,16,64]{0,2,1:T(8,128)(2,1)}, u32[]{:S(2)}) copy-start(bf16[512,16,64]{0,2,1:T(8,128)(2,1)} %get-tuple-element.257) | copy-start | bytes 3145732 | tf_op jit(solution)/shard_map/while/body/eval_jaxpr/cond
  207.0 1.0 copy-start.4
  210.7 7.5 %copy-start.1 = (f32[16,256,64]{1,2,0:T(8,128)S(1)}, f32[16,256,64]{1,2,0:T(8,128)}, u32[]{:S(2)}) copy-start(f32[16,256,64]{1,2,0:T(8,128)} %get-tuple-element.248) | copy-start | bytes 3145732 | tf_op jit(solution)/shard_map/while/body/eval_jaxpr/cond
  210.7 7.5 %copy-start.6 = (bf16[512,16,64]{0,2,1:T(8,128)(2,1)S(1)}, bf16[512,16,64]{0,2,1:T(8,128)(2,1)}, u32[]{:S(2)}) copy-start(bf16[512,16,64]{0,2,1:T(8,128)(2,1)} %get-tuple-element.249) | copy-start | bytes 3145732 | tf_op jit(solution)/shard_map/while/body/eval_jaxpr/cond
  221.4 1.0 copy-start.2
  240.0 7.5 %copy-start.3 = (f32[16,256,64]{1,2,0:T(8,128)S(1)}, f32[16,256,64]{1,2,0:T(8,128)}, u32[]{:S(2)}) copy-start(f32[16,256,64]{1,2,0:T(8,128)} %get-tuple-element.256) | copy-start | bytes 3145732 | tf_op jit(solution)/shard_map/while/body/eval_jaxpr/cond
  240.0 7.5 %copy-start.5 = (bf16[512,16,64]{0,2,1:T(8,128)(2,1)S(1)}, bf16[512,16,64]{0,2,1:T(8,128)(2,1)}, u32[]{:S(2)}) copy-start(bf16[512,16,64]{0,2,1:T(8,128)(2,1)} %get-tuple-element.257) | copy-start | bytes 3145732 | tf_op jit(solution)/shard_map/while/body/eval_jaxpr/cond
  250.7 1.0 copy-start.4
  254.4 7.5 %copy-start.1 = (f32[16,256,64]{1,2,0:T(8,128)S(1)}, f32[16,256,64]{1,2,0:T(8,128)}, u32[]{:S(2)}) copy-start(f32[16,256,64]{1,2,0:T(8,128)} %get-tuple-element.248) | copy-start | bytes 3145732 | tf_op jit(solution)/shard_map/while/body/eval_jaxpr/cond
  254.4 7.5 %copy-start.6 = (bf16[512,16,64]{0,2,1:T(8,128)(2,1)S(1)}, bf16[512,16,64]{0,2,1:T(8,128)(2,1)}, u32[]{:S(2)}) copy-start(bf16[512,16,64]{0,2,1:T(8,128)(2,1)} %get-tuple-element.249) | copy-start | bytes 3145732 | tf_op jit(solution)/shard_map/while/body/eval_jaxpr/cond
  265.1 1.0 copy-start.2
Sparse Core Ops, SparseCore 0:
  81.6 49.5 all-gather.2
  133.3 47.6 all-gather.4
